TPU v7x, 32 devices: a whole 2x2x4 slice. The times are simulated.
32 devices in a mesh: groups: 2 (over y), ctx: 16 (over z, x, core).
Axes of the slice: x: 2, y: 2, z: 4, core: 2. Of those that a mesh axis runs over, the one named last changes fastest.
Arguments:
- query_rows: bfloat16 [4096, 2560], P(('groups', 'ctx')), parts along dimension 0, may hold values from -211 to 211
- key_rows: bfloat16 [4096, 2560], P(('groups', 'ctx')), parts along dimension 0, may hold values from -6.2 to 6.2
- value_rows: bfloat16 [4096, 2560], P(('groups', 'ctx')), parts along dimension 0, may hold values from -6 to 6
- out_grad: bfloat16 [4096, 2560], P(('groups', 'ctx')), parts along dimension 0, may hold values from -6 to 6
- selected: int32 [32, 8], P('groups'), parts along dimension 0, may hold values from 0 to 15, as said below
Outputs:
- attended: bfloat16 [4096, 2560], P(('groups', 'ctx')), parts along dimension 0
- grad_query: bfloat16 [4096, 2560], P(('groups', 'ctx')), parts along dimension 0
- grad_key: bfloat16 [4096, 2560], P(('groups', 'ctx')), parts along dimension 0
- grad_value: bfloat16 [4096, 2560], P(('groups', 'ctx')), parts along dimension 0
- pooled_key_grad: float32 [64, 2560], P(('groups', 'ctx')), parts along dimension 0
- pooled_value_grad: float32 [64, 2560], P(('groups', 'ctx')), parts along dimension 0
There are 2 independent parts, one for each index of `groups`. A program takes and returns all parts, laid end to end along the dimension named above; each array names one. Nothing has to cross between parts.
Inputs may be any that keep to these rules, and one draw needn't show every extreme that they name: `selected`: each row names 8 different tiles.
All inputs are finite; a program needn't handle non-finite values.
Results may differ from a plain program's by a relative error of at most 0.029.
Values may be sent and summed in bfloat16 or wider, within the bound.
A program may use at most 192 MiB of HBM per device.

v0:
```python
import functools
import math

import jax
import jax.numpy as jnp
from jax import lax
from jax.experimental import pallas as pl
from jax.experimental.pallas import tpu as pltpu
from jax.sharding import PartitionSpec as P

HEADS = 20
HEAD_DIM = 128
TILE = 128
POOL = 64
SEL = 8
CORES = 2
PAIR = 2


def pooled(rows):
    return jnp.mean(rows.astype(jnp.float32).reshape(-1, POOL, rows.shape[1]), axis=1).astype(
        jnp.bfloat16
    )


def contract(left, right, left_dim, right_dim):
    return lax.dot_general(
        left, right, (((left_dim,), (right_dim,)), ((), ())), preferred_element_type=jnp.float32
    )


def attend(queries, grads_out, keys_all, values_all):
    scaling = HEAD_DIM ** (-0.5)
    out_parts, query_parts, key_parts, value_parts = ([], [], [], [])
    for head in range(HEADS):
        lower = head * HEAD_DIM
        upper = lower + HEAD_DIM
        head_query = queries[:, lower:upper]
        head_grad = grads_out[:, lower:upper]
        head_key = keys_all[:, lower:upper]
        head_value = values_all[:, lower:upper]
        scores = contract(head_query, head_key, 1, 1) * scaling
        summit = jnp.max(scores, axis=-1, keepdims=True)
        raised = jnp.exp(scores - summit)
        weights = raised / jnp.sum(raised, axis=-1, keepdims=True)
        rounded = weights.astype(jnp.bfloat16)
        out_rows = jnp.dot(rounded, head_value, preferred_element_type=jnp.float32).astype(
            jnp.bfloat16
        )
        row_dots = jnp.sum(
            head_grad.astype(jnp.float32) * out_rows.astype(jnp.float32), axis=-1, keepdims=True
        )
        prob_grad = contract(head_grad, head_value, 1, 1)
        score_grad = (weights * (prob_grad - row_dots)).astype(jnp.bfloat16)
        query_grad = jnp.dot(score_grad, head_key, preferred_element_type=jnp.float32) * scaling
        key_terms = contract(score_grad, head_query, 0, 0) * scaling
        value_terms = contract(rounded, head_grad, 0, 0)
        out_parts.append(out_rows)
        query_parts.append(query_grad.astype(jnp.bfloat16))
        key_parts.append(key_terms)
        value_parts.append(value_terms)
    return (
        jnp.concatenate(out_parts, axis=1),
        jnp.concatenate(query_parts, axis=1),
        jnp.concatenate(key_parts, axis=1),
        jnp.concatenate(value_parts, axis=1),
    )


def package(tiles_in, pooled_in, devices, spread):
    tiles_here, tile_len, columns = tiles_in.shape
    per_tile = tile_len // POOL
    split_rows = tiles_in.reshape(tiles_here, devices, spread, columns)
    copies = jnp.broadcast_to(
        pooled_in.reshape(tiles_here, 1, per_tile, columns),
        (tiles_here, devices, per_tile, columns),
    )
    return jnp.concatenate([split_rows, copies], axis=2).reshape(
        tiles_here, devices * (spread + per_tile), columns
    )


def listed_shards(query_rows, key_rows, value_rows, out_grad, selected):
    height, columns = query_rows.shape
    devices = lax.axis_size("ctx")
    tiles_here = height // TILE
    spread = TILE // devices
    own_keys = pooled(key_rows)
    own_values = pooled(value_rows)
    key_tiles = key_rows.reshape(tiles_here, TILE, columns)
    value_tiles = value_rows.reshape(tiles_here, TILE, columns)
    joined_keys, joined_values = (
        lax.all_to_all(
            package(key_tiles, own_keys, devices, spread),
            "ctx",
            split_axis=1,
            concat_axis=0,
            tiled=True,
        ),
        lax.all_to_all(
            package(value_tiles, own_values, devices, spread),
            "ctx",
            split_axis=1,
            concat_axis=0,
            tiled=True,
        ),
    )
    held_keys = joined_keys[:, :spread]
    held_values = joined_values[:, :spread]
    pool_keys = joined_keys[:, spread:].reshape(-1, columns)
    pool_values = joined_values[:, spread:].reshape(-1, columns)
    comp_count = pool_keys.shape[0]
    got_keys, got_values = (
        lax.all_to_all(held_keys[selected], "ctx", split_axis=0, concat_axis=2, tiled=True),
        lax.all_to_all(held_values[selected], "ctx", split_axis=0, concat_axis=2, tiled=True),
    )
    fine_keys = got_keys.reshape(tiles_here, SEL * TILE, columns)
    fine_values = got_values.reshape(tiles_here, SEL * TILE, columns)
    out_tiles, query_tiles, key_listed, value_listed = ([], [], [], [])
    keys_all = jnp.concatenate([pool_keys, fine_keys[0]], axis=0)
    values_all = jnp.concatenate([pool_values, fine_values[0]], axis=0)
    out_rows, query_grad, key_terms, value_terms = attend(
        query_rows, out_grad, keys_all, values_all
    )
    out_tiles.append(out_rows)
    query_tiles.append(query_grad)
    coarse_keys = key_terms[:comp_count]
    coarse_values = value_terms[:comp_count]
    key_listed.append(key_terms[comp_count:].astype(jnp.bfloat16))
    value_listed.append(value_terms[comp_count:].astype(jnp.bfloat16))
    own_coarse_keys, own_coarse_values = (
        lax.psum_scatter(coarse_keys, "ctx", scatter_dimension=0, tiled=True),
        lax.psum_scatter(coarse_values, "ctx", scatter_dimension=0, tiled=True),
    )
    listed_keys = jnp.stack(key_listed).reshape(tiles_here * SEL, devices, spread, columns)
    listed_values = jnp.stack(value_listed).reshape(tiles_here * SEL, devices, spread, columns)
    back_keys, back_values = (
        lax.all_to_all(listed_keys, "ctx", split_axis=1, concat_axis=0, tiled=True),
        lax.all_to_all(listed_values, "ctx", split_axis=1, concat_axis=0, tiled=True),
    )
    tile_ids = jnp.arange(selected.shape[0], dtype=jnp.int32)[:, None]
    member = (selected.reshape(1, -1) == tile_ids).astype(jnp.bfloat16)
    entries = member.shape[1]
    sum_keys = jnp.dot(
        member, back_keys.reshape(entries, spread * columns), preferred_element_type=jnp.float32
    )
    sum_values = jnp.dot(
        member, back_values.reshape(entries, spread * columns), preferred_element_type=jnp.float32
    )
    held_key_grad = sum_keys.astype(jnp.bfloat16).reshape(devices, tiles_here, spread, columns)
    held_value_grad = sum_values.astype(jnp.bfloat16).reshape(devices, tiles_here, spread, columns)
    owned_keys, owned_values = (
        lax.all_to_all(held_key_grad, "ctx", split_axis=0, concat_axis=2, tiled=True),
        lax.all_to_all(held_value_grad, "ctx", split_axis=0, concat_axis=2, tiled=True),
    )
    grad_key = (
        owned_keys.reshape(height, columns).astype(jnp.float32)
        + jnp.repeat(own_coarse_keys, POOL, axis=0) / POOL
    ).astype(jnp.bfloat16)
    grad_value = (
        owned_values.reshape(height, columns).astype(jnp.float32)
        + jnp.repeat(own_coarse_values, POOL, axis=0) / POOL
    ).astype(jnp.bfloat16)
    attended = out_tiles[0]
    grad_query = query_tiles[0]
    return (attended, grad_query, grad_key, grad_value, own_coarse_keys, own_coarse_values)


SLOTS = 2


def split_places(devices):
    cores = CORES * PAIR
    levels = devices // cores
    extra = HEADS // levels
    return cores, levels, extra


def owner_of(head):
    cores = CORES * PAIR
    level = head // (cores + 1)
    j = head % (cores + 1)
    spare = j // cores
    extra_at = CORES * (level % PAIR) + CORES - 1
    return level * cores + (1 - spare) * j + spare * extra_at, spare


def holds_two(me):
    cores = CORES * PAIR
    level = me // cores
    return me % cores == CORES * (level % PAIR) + CORES - 1


def meet(devices, me):
    barrier = pltpu.get_barrier_semaphore()
    for k in range(1, devices):
        pl.semaphore_signal(
            barrier,
            inc=1,
            device_id={"ctx": lax.rem(me + k, devices)},
            device_id_type=pl.DeviceIdType.MESH,
        )
    pl.semaphore_wait(barrier, devices - 1)


def spread_kernel(devices, k_ref, v_ref, q_ref, g_ref, rk_ref, rv_ref, rq_ref, rg_ref,
                  send_sem, recv_sem, own_sem):
    me = lax.axis_index("ctx")
    per_level = HEADS // (devices // (CORES * PAIR))
    meet(devices, me)
    two = holds_two(me)
    first = (me // (CORES * PAIR) + 1) * per_level
    rows = pl.ds(pl.multiple_of(me * TILE, TILE), TILE)
    sources = (k_ref, v_ref, q_ref, g_ref)
    targets = (rk_ref, rv_ref, rq_ref, rg_ref)
    for pair in (0, 2):

        def step(i, carry):
            head = lax.rem(first + i, HEADS)
            owner, slot = owner_of(head)
            columns = pl.ds(pl.multiple_of(head * HEAD_DIM, HEAD_DIM), HEAD_DIM)
            for a in (pair, pair + 1):
                src = sources[a].at[:, columns]
                dst = targets[a].at[slot, rows, :]

                @pl.when(owner != me)
                def _():
                    pltpu.make_async_remote_copy(
                        src_ref=src,
                        dst_ref=dst,
                        send_sem=send_sem.at[a],
                        recv_sem=recv_sem.at[a, slot],
                        device_id={"ctx": owner},
                        device_id_type=pl.DeviceIdType.MESH,
                    ).start()

                @pl.when(owner == me)
                def _():
                    pltpu.make_async_copy(src, dst, own_sem.at[a, slot]).start()

            return carry

        lax.fori_loop(0, HEADS, step, 0)
    others = (devices - 1) * TILE

    def wait(slot):
        for a in range(4):
            got = targets[a].at[slot, pl.ds(0, others), :]
            pltpu.make_async_copy(got, got, recv_sem.at[a, slot]).wait()
            own = targets[a].at[slot, rows, :]
            pltpu.make_async_copy(own, own, own_sem.at[a, slot]).wait()

    wait(0)

    @pl.when(two)
    def _():
        wait(1)
        for a in range(4):
            sent = sources[a].at[:, pl.ds(0, (HEADS - 2) * HEAD_DIM)]
            pltpu.make_async_copy(sent, sent, send_sem.at[a]).wait()

    @pl.when(jnp.logical_not(two))
    def _():
        for a in range(4):
            sent = sources[a].at[:, pl.ds(0, (HEADS - 1) * HEAD_DIM)]
            pltpu.make_async_copy(sent, sent, send_sem.at[a]).wait()


def spread(arrays, devices):
    shape = jax.ShapeDtypeStruct((SLOTS, devices * TILE, HEAD_DIM), jnp.bfloat16)
    return pl.pallas_call(
        functools.partial(spread_kernel, devices),
        out_shape=[shape] * 4,
        in_specs=[pl.BlockSpec(memory_space=pl.ANY)] * 4,
        out_specs=[pl.BlockSpec(memory_space=pl.ANY)] * 4,
        scratch_shapes=[
            pltpu.SemaphoreType.DMA((4,)),
            pltpu.SemaphoreType.DMA((4, SLOTS)),
            pltpu.SemaphoreType.DMA((4, SLOTS)),
        ],
        compiler_params=pltpu.CompilerParams(collective_id=0, has_side_effects=True),
        name="spread",
    )(*arrays)


def collect_kernel(devices, o_ref, dq_ref, dk_ref, dv_ref, c_ref,
                   ro_ref, rq_ref, rk_ref, rv_ref, rc_ref, send_sem, recv_sem, own_sem):
    me = lax.axis_index("ctx")
    cores = CORES * PAIR
    meet(devices, me)
    two = holds_two(me)
    level = me // cores
    sources = (o_ref, dq_ref, dk_ref, dv_ref)
    targets = (ro_ref, rq_ref, rk_ref, rv_ref)

    def parts(slot, tile):
        head = level * (cores + 1) + (1 - slot) * (me % cores) + slot * cores
        rows = pl.ds(pl.multiple_of(tile * TILE, TILE), TILE)
        columns = pl.ds(pl.multiple_of(head * HEAD_DIM, HEAD_DIM), HEAD_DIM)
        for a in range(4):
            yield a, sources[a].at[slot, rows, :], targets[a].at[:, columns]
        yield 4, c_ref.at[slot, tile], rc_ref.at[head]

    def send(slot):
        def step(i, carry):
            tile = lax.rem(me + 1 + i, devices)
            for a, src, dst in parts(slot, tile):
                pltpu.make_async_remote_copy(
                    src_ref=src,
                    dst_ref=dst,
                    send_sem=send_sem.at[a, slot],
                    recv_sem=recv_sem.at[a],
                    device_id={"ctx": tile},
                    device_id_type=pl.DeviceIdType.MESH,
                ).start()
            return carry

        lax.fori_loop(0, devices - 1, step, 0)
        for a, src, dst in parts(slot, me):
            pltpu.make_async_copy(src, dst, own_sem.at[a, slot]).start()

    def sent(slot):
        for a, src, dst in parts(slot, me):
            pltpu.make_async_copy(src, dst, own_sem.at[a, slot]).wait()
        for a in range(4):
            gone = sources[a].at[slot, pl.ds(0, (devices - 1) * TILE), :]
            pltpu.make_async_copy(gone, gone, send_sem.at[a, slot]).wait()
        gone = c_ref.at[slot, pl.ds(0, devices - 1)]
        pltpu.make_async_copy(gone, gone, send_sem.at[4, slot]).wait()

    def got(heads):
        for a in range(4):
            here = targets[a].at[:, pl.ds(0, heads * HEAD_DIM)]
            pltpu.make_async_copy(here, here, recv_sem.at[a]).wait()
        here = rc_ref.at[pl.ds(0, heads)]
        pltpu.make_async_copy(here, here, recv_sem.at[4]).wait()

    send(0)

    @pl.when(two)
    def _():
        send(1)
        sent(1)
        got(HEADS - 2)

    @pl.when(jnp.logical_not(two))
    def _():
        got(HEADS - 1)

    sent(0)


def collect(arrays, devices):
    flat = jax.ShapeDtypeStruct((TILE, HEADS * HEAD_DIM), jnp.bfloat16)
    coarse = jax.ShapeDtypeStruct((HEADS, 8, HEAD_DIM), jnp.float32)
    return pl.pallas_call(
        functools.partial(collect_kernel, devices),
        out_shape=[flat] * 4 + [coarse],
        in_specs=[pl.BlockSpec(memory_space=pl.ANY)] * 5,
        out_specs=[pl.BlockSpec(memory_space=pl.ANY)] * 5,
        scratch_shapes=[
            pltpu.SemaphoreType.DMA((5, SLOTS)),
            pltpu.SemaphoreType.DMA((5,)),
            pltpu.SemaphoreType.DMA((5, SLOTS)),
        ],
        compiler_params=pltpu.CompilerParams(collective_id=1, has_side_effects=True),
        name="collect",
    )(*arrays)


def whole_head_kernel(place_ref, count_ref, k_ref, v_ref, q_ref, g_ref,
                      o_ref, dq_ref, dk_ref, dv_ref, c_ref, joined, keys_t, values_t, total):
    tokens = k_ref.shape[0]
    tiles = tokens // TILE
    pools = tokens // POOL
    scaling = HEAD_DIM ** (-0.5)
    rate = scaling * math.log2(math.e)

    @pl.when(pl.program_id(0) < count_ref[0])
    def _():
        for ref, at, turned in ((k_ref, 0, keys_t), (v_ref, HEAD_DIM, values_t)):
            rows = ref[...]
            wide = rows.astype(jnp.float32)
            means = jnp.sum(wide.reshape(pools, POOL, HEAD_DIM), axis=1) * (1.0 / POOL)
            means = means.astype(jnp.bfloat16)
            joined[:tokens, at : at + HEAD_DIM] = rows
            joined[tokens:, at : at + HEAD_DIM] = means
            turned[:, :tokens] = rows.T
            turned[:, tokens:] = means.T
        total[...] = jnp.zeros_like(total)

        def tile_step(t, carry):
            rows = pl.ds(pl.multiple_of(t * TILE, TILE), TILE)
            query = q_ref[rows, :]
            grad = g_ref[rows, :]
            blank = jnp.zeros_like(query)
            paired = jnp.concatenate(
                [
                    jnp.concatenate([query, blank], axis=1),
                    jnp.concatenate([blank, grad], axis=1),
                ],
                axis=0,
            )
            starts = [pl.multiple_of(place_ref[t * SEL + j] * TILE, TILE) for j in range(SEL)]
            listed = jnp.concatenate(
                [joined[pl.ds(s, TILE), :] for s in starts] + [joined[tokens:, :]], axis=0
            )
            both = contract(listed, paired, 1, 1)
            scores = both[:, :TILE]
            prob_grad = both[:, TILE:]
            summit = jnp.max(scores, axis=0, keepdims=True)
            raised = jnp.exp2((scores - summit) * rate)
            scale = 1.0 / jnp.sum(raised, axis=0, keepdims=True)
            dots = jnp.sum(raised * prob_grad, axis=0, keepdims=True) * scale
            weights = raised * scale
            score_grad = (weights * (prob_grad - dots)).astype(jnp.bfloat16)
            rounded = weights.astype(jnp.bfloat16)
            listed_kt = jnp.concatenate(
                [keys_t[:, pl.ds(s, TILE)] for s in starts] + [keys_t[:, tokens:]], axis=1
            )
            listed_vt = jnp.concatenate(
                [values_t[:, pl.ds(s, TILE)] for s in starts] + [values_t[:, tokens:]], axis=1
            )
            out_t = jnp.dot(listed_vt, rounded, preferred_element_type=jnp.float32)
            dq_t = jnp.dot(listed_kt, score_grad, preferred_element_type=jnp.float32) * scaling
            o_ref[rows, :] = out_t.T.astype(jnp.bfloat16)
            dq_ref[rows, :] = dq_t.T.astype(jnp.bfloat16)
            terms = jnp.dot(
                jnp.concatenate([score_grad, rounded], axis=1),
                paired,
                preferred_element_type=jnp.float32,
            )
            for j, s in enumerate(starts):
                total[pl.ds(s, TILE), :] += terms[j * TILE : (j + 1) * TILE]
            total[tokens:, :] += terms[SEL * TILE :]
            return carry

        lax.fori_loop(0, tiles, tile_step, 0)
        per_tile = TILE // POOL
        for ref, at, factor in ((dk_ref, 0, scaling), (dv_ref, HEAD_DIM, 1.0)):
            coarse = total[tokens:, at : at + HEAD_DIM] * factor
            fine = total[:tokens, at : at + HEAD_DIM] * factor
            fine = fine.reshape(pools, POOL, HEAD_DIM) + (coarse * (1.0 / POOL))[:, None, :]
            ref[...] = fine.reshape(tokens, HEAD_DIM).astype(jnp.bfloat16)
            start = 0 if at == 0 else per_tile
            for tile in range(tiles):
                c_ref[tile, start : start + per_tile, :] = coarse[
                    tile * per_tile : (tile + 1) * per_tile
                ]


def whole_heads(place, count, rk, rv, rq, rg):
    tokens = rk.shape[1]
    tiles = tokens // TILE
    pools = tokens // POOL
    used = lambda s, place, count: (jnp.minimum(s, count[0] - 1), 0, 0)
    here = lambda s, place, count: (s, 0, 0)
    rows = jax.ShapeDtypeStruct((SLOTS, tokens, HEAD_DIM), jnp.bfloat16)
    block = (None, tokens, HEAD_DIM)
    return pl.pallas_call(
        whole_head_kernel,
        grid_spec=pltpu.PrefetchScalarGridSpec(
            num_scalar_prefetch=2,
            grid=(SLOTS,),
            in_specs=[pl.BlockSpec(block, used)] * 4,
            out_specs=[pl.BlockSpec(block, here)] * 4
            + [pl.BlockSpec((None, tiles, 8, HEAD_DIM), lambda s, place, count: (s, 0, 0, 0))],
            scratch_shapes=[
                pltpu.VMEM((tokens + pools, 2 * HEAD_DIM), jnp.bfloat16),
                pltpu.VMEM((HEAD_DIM, tokens + pools), jnp.bfloat16),
                pltpu.VMEM((HEAD_DIM, tokens + pools), jnp.bfloat16),
                pltpu.VMEM((tokens + pools, 2 * HEAD_DIM), jnp.float32),
            ],
        ),
        out_shape=[rows] * 4
        + [jax.ShapeDtypeStruct((SLOTS, tiles, 8, HEAD_DIM), jnp.float32)],
        name="whole_heads",
    )(place, count, rk, rv, rq, rg)


def exchange_shards(query_rows, key_rows, value_rows, out_grad, selected):
    devices = lax.axis_size("ctx")
    me = lax.axis_index("ctx")
    rk, rv, rq, rg = spread((key_rows, value_rows, query_rows, out_grad), devices)
    count = jnp.where(holds_two(me), 2, 1).astype(jnp.int32).reshape(1)
    out, dq, dk, dv, coarse = whole_heads(selected.reshape(-1), count, rk, rv, rq, rg)
    out, dq, dk, dv, coarse = collect((out, dq, dk, dv, coarse), devices)
    per_tile = TILE // POOL
    flat = lambda part: part.transpose(1, 0, 2).reshape(per_tile, HEADS * HEAD_DIM)
    return (
        out,
        dq,
        dk,
        dv,
        flat(coarse[:, :per_tile]),
        flat(coarse[:, per_tile : 2 * per_tile]),
    )


def shards(query_rows, key_rows, value_rows, out_grad, selected):
    devices = lax.axis_size("ctx")
    fits = devices == 4 * CORES * PAIR and query_rows.shape[0] == TILE
    chosen = exchange_shards if fits else listed_shards
    return chosen(query_rows, key_rows, value_rows, out_grad, selected)


def solution(mesh):
    in_specs = (
        P(("groups", "ctx"), None),
        P(("groups", "ctx"), None),
        P(("groups", "ctx"), None),
        P(("groups", "ctx"), None),
        P("groups", None),
    )
    out_specs = (
        P(("groups", "ctx"), None),
        P(("groups", "ctx"), None),
        P(("groups", "ctx"), None),
        P(("groups", "ctx"), None),
        P(("groups", "ctx"), None),
        P(("groups", "ctx"), None),
    )
    return jax.shard_map(shards, mesh=mesh, in_specs=in_specs, out_specs=out_specs, check_vma=False)
```

profile of v0, /device:TPU:11, one launch (start us, length us, event | category | flops | bytes accessed | tf_op | source)
XLA Modules:
  0.0 181.6 jit_solution(5836080762726280438)
XLA Ops:
  0.7 0.0 copy-start.3
  0.7 0.7 copy-done.3
  1.4 0.1 copy.12
  1.4 0.6 reshape.24.place_ref
  2.0 61.8 %spread.1 = (bf16[2,2048,128]{2,1,0:T(8,128)(2,1)}, bf16[2,2048,128]{2,1,0:T(8,128)(2,1)}, bf16[2,2048,128]{2,1,0:T(8,128)(2,1)}, bf16[2,2048,128]{2,1,0:T(8,128)(2,1)}) custom-call(bf16[128,2560]{1,0:T(8,128)(2,1)} %k_ref.1, bf16[128,2560]{1,0:T(8,128)(2,1)} %v_ref.1, bf16[128,2560]{1,0:T(8,128)(2,1)} %q_ref.1, bf16[128,2560]{1,0:T(8,128)(2,1)} %g_ref.1), custom_call_target="tpu_custom_call" | custom-call | tf_op jit(solution)/shard_map/spread/pallas_call | solution.py:271
  63.9 47.0 %whole_heads.1 = (bf16[2,2048,128]{2,1,0:T(8,128)(2,1)}, bf16[2,2048,128]{2,1,0:T(8,128)(2,1)}, bf16[2,2048,128]{2,1,0:T(8,128)(2,1)}, bf16[2,2048,128]{2,1,0:T(8,128)(2,1)}, f32[2,16,8,128]{3,2,1,0:T(8,128)}) custom-call(s32[128]{0:T(128)} %reshape.24.place_ref, s32[1]{0:T(128)} %bitcast.count_ref, bf16[2,2048,128]{2,1,0:T(8,128)(2,1)} %get-tuple-element.20.k_ref, ...), custom_call_target="tpu_custom_call" | custom-call | tf_op jit(solution)/shard_map/whole_heads/pallas_call | solution.py:460
  110.9 63.5 %collect.1 = (bf16[128,2560]{1,0:T(8,128)(2,1)}, bf16[128,2560]{1,0:T(8,128)(2,1)}, bf16[128,2560]{1,0:T(8,128)(2,1)}, bf16[128,2560]{1,0:T(8,128)(2,1)}, f32[20,8,128]{2,1,0:T(8,128)}) custom-call(bf16[2,2048,128]{2,1,0:T(8,128)(2,1)} %get-tuple-element.24.o_ref, bf16[2,2048,128]{2,1,0:T(8,128)(2,1)} %get-tuple-element.25.dq_ref, ...), custom_call_target="tpu_custom_call" | custom-call | tf_op jit(solution)/shard_map/collect/pallas_call | solution.py:356
  174.5 1.6 slice_bitcast_fusion
  176.0 0.0 copy-start.2
  176.0 2.0 %copy.17 = bf16[128,2560]{1,0:T(8,128)(2,1)} copy(bf16[128,2560]{1,0:T(8,128)(2,1)} %get-tuple-element.42) | data formatting | bytes 1310720
  178.1 0.0 copy-done.2
  178.1 0.0 copy-start.1
  178.1 0.8 copy.18
  178.9 0.5 copy-done.1
  179.4 0.0 copy-start
  179.4 0.8 copy.19
  180.2 0.5 copy-done
  180.7 0.8 copy.20
Async XLA Ops:
  0.7 0.7 copy-start.3
  176.0 2.0 %copy-start.2 = (bf16[128,2560]{1,0:T(8,128)(2,1)S(1)}, bf16[128,2560]{1,0:T(8,128)(2,1)}, u32[]{:S(2)}) copy-start(bf16[128,2560]{1,0:T(8,128)(2,1)} %get-tuple-element.43) | copy-start | bytes 1966084
  178.1 1.3 copy-start.1
  179.4 1.3 copy-start
where the time goes:
time: 182 us
  Pallas kernels  172 us (95%)
  local copies, waits for them, and re-layouts  8.45 us (5%)
    pallas_call x1, Pallas kernels, collect(): pl.pallas_call(functools.partial(collect_kernel, devices), out_shape=[fla...  63.5 us
    pallas_call x1, Pallas kernels, spread(): pl.pallas_call(functools.partial(spread_kernel, devices), out_shape=[shap...  61.8 us
    pallas_call x1, Pallas kernels, whole_heads(): pl.pallas_call(whole_head_kernel, grid_spec=pltpu.PrefetchScalarGridSpec(...  47 us
    unnamed x13, local copies, waits for them, and re-layouts  6.26 us

commit v1 on v0

v1 whole, which is shorter than its diff:
```python
import functools
import math

import jax
import jax.numpy as jnp
from jax import lax
from jax.experimental import pallas as pl
from jax.experimental.pallas import tpu as pltpu
from jax.sharding import PartitionSpec as P

HEADS = 20
HEAD_DIM = 128
TILE = 128
POOL = 64
SEL = 8
CORES = 2
PAIR = 2


def pooled(rows):
    return jnp.mean(rows.astype(jnp.float32).reshape(-1, POOL, rows.shape[1]), axis=1).astype(
        jnp.bfloat16
    )


def contract(left, right, left_dim, right_dim):
    return lax.dot_general(
        left, right, (((left_dim,), (right_dim,)), ((), ())), preferred_element_type=jnp.float32
    )


def attend(queries, grads_out, keys_all, values_all):
    scaling = HEAD_DIM ** (-0.5)
    out_parts, query_parts, key_parts, value_parts = ([], [], [], [])
    for head in range(HEADS):
        lower = head * HEAD_DIM
        upper = lower + HEAD_DIM
        head_query = queries[:, lower:upper]
        head_grad = grads_out[:, lower:upper]
        head_key = keys_all[:, lower:upper]
        head_value = values_all[:, lower:upper]
        scores = contract(head_query, head_key, 1, 1) * scaling
        summit = jnp.max(scores, axis=-1, keepdims=True)
        raised = jnp.exp(scores - summit)
        weights = raised / jnp.sum(raised, axis=-1, keepdims=True)
        rounded = weights.astype(jnp.bfloat16)
        out_rows = jnp.dot(rounded, head_value, preferred_element_type=jnp.float32).astype(
            jnp.bfloat16
        )
        row_dots = jnp.sum(
            head_grad.astype(jnp.float32) * out_rows.astype(jnp.float32), axis=-1, keepdims=True
        )
        prob_grad = contract(head_grad, head_value, 1, 1)
        score_grad = (weights * (prob_grad - row_dots)).astype(jnp.bfloat16)
        query_grad = jnp.dot(score_grad, head_key, preferred_element_type=jnp.float32) * scaling
        key_terms = contract(score_grad, head_query, 0, 0) * scaling
        value_terms = contract(rounded, head_grad, 0, 0)
        out_parts.append(out_rows)
        query_parts.append(query_grad.astype(jnp.bfloat16))
        key_parts.append(key_terms)
        value_parts.append(value_terms)
    return (
        jnp.concatenate(out_parts, axis=1),
        jnp.concatenate(query_parts, axis=1),
        jnp.concatenate(key_parts, axis=1),
        jnp.concatenate(value_parts, axis=1),
    )


def package(tiles_in, pooled_in, devices, spread):
    tiles_here, tile_len, columns = tiles_in.shape
    per_tile = tile_len // POOL
    split_rows = tiles_in.reshape(tiles_here, devices, spread, columns)
    copies = jnp.broadcast_to(
        pooled_in.reshape(tiles_here, 1, per_tile, columns),
        (tiles_here, devices, per_tile, columns),
    )
    return jnp.concatenate([split_rows, copies], axis=2).reshape(
        tiles_here, devices * (spread + per_tile), columns
    )


def listed_shards(query_rows, key_rows, value_rows, out_grad, selected):
    height, columns = query_rows.shape
    devices = lax.axis_size("ctx")
    tiles_here = height // TILE
    spread = TILE // devices
    own_keys = pooled(key_rows)
    own_values = pooled(value_rows)
    key_tiles = key_rows.reshape(tiles_here, TILE, columns)
    value_tiles = value_rows.reshape(tiles_here, TILE, columns)
    joined_keys, joined_values = (
        lax.all_to_all(
            package(key_tiles, own_keys, devices, spread),
            "ctx",
            split_axis=1,
            concat_axis=0,
            tiled=True,
        ),
        lax.all_to_all(
            package(value_tiles, own_values, devices, spread),
            "ctx",
            split_axis=1,
            concat_axis=0,
            tiled=True,
        ),
    )
    held_keys = joined_keys[:, :spread]
    held_values = joined_values[:, :spread]
    pool_keys = joined_keys[:, spread:].reshape(-1, columns)
    pool_values = joined_values[:, spread:].reshape(-1, columns)
    comp_count = pool_keys.shape[0]
    got_keys, got_values = (
        lax.all_to_all(held_keys[selected], "ctx", split_axis=0, concat_axis=2, tiled=True),
        lax.all_to_all(held_values[selected], "ctx", split_axis=0, concat_axis=2, tiled=True),
    )
    fine_keys = got_keys.reshape(tiles_here, SEL * TILE, columns)
    fine_values = got_values.reshape(tiles_here, SEL * TILE, columns)
    out_tiles, query_tiles, key_listed, value_listed = ([], [], [], [])
    keys_all = jnp.concatenate([pool_keys, fine_keys[0]], axis=0)
    values_all = jnp.concatenate([pool_values, fine_values[0]], axis=0)
    out_rows, query_grad, key_terms, value_terms = attend(
        query_rows, out_grad, keys_all, values_all
    )
    out_tiles.append(out_rows)
    query_tiles.append(query_grad)
    coarse_keys = key_terms[:comp_count]
    coarse_values = value_terms[:comp_count]
    key_listed.append(key_terms[comp_count:].astype(jnp.bfloat16))
    value_listed.append(value_terms[comp_count:].astype(jnp.bfloat16))
    own_coarse_keys, own_coarse_values = (
        lax.psum_scatter(coarse_keys, "ctx", scatter_dimension=0, tiled=True),
        lax.psum_scatter(coarse_values, "ctx", scatter_dimension=0, tiled=True),
    )
    listed_keys = jnp.stack(key_listed).reshape(tiles_here * SEL, devices, spread, columns)
    listed_values = jnp.stack(value_listed).reshape(tiles_here * SEL, devices, spread, columns)
    back_keys, back_values = (
        lax.all_to_all(listed_keys, "ctx", split_axis=1, concat_axis=0, tiled=True),
        lax.all_to_all(listed_values, "ctx", split_axis=1, concat_axis=0, tiled=True),
    )
    tile_ids = jnp.arange(selected.shape[0], dtype=jnp.int32)[:, None]
    member = (selected.reshape(1, -1) == tile_ids).astype(jnp.bfloat16)
    entries = member.shape[1]
    sum_keys = jnp.dot(
        member, back_keys.reshape(entries, spread * columns), preferred_element_type=jnp.float32
    )
    sum_values = jnp.dot(
        member, back_values.reshape(entries, spread * columns), preferred_element_type=jnp.float32
    )
    held_key_grad = sum_keys.astype(jnp.bfloat16).reshape(devices, tiles_here, spread, columns)
    held_value_grad = sum_values.astype(jnp.bfloat16).reshape(devices, tiles_here, spread, columns)
    owned_keys, owned_values = (
        lax.all_to_all(held_key_grad, "ctx", split_axis=0, concat_axis=2, tiled=True),
        lax.all_to_all(held_value_grad, "ctx", split_axis=0, concat_axis=2, tiled=True),
    )
    grad_key = (
        owned_keys.reshape(height, columns).astype(jnp.float32)
        + jnp.repeat(own_coarse_keys, POOL, axis=0) / POOL
    ).astype(jnp.bfloat16)
    grad_value = (
        owned_values.reshape(height, columns).astype(jnp.float32)
        + jnp.repeat(own_coarse_values, POOL, axis=0) / POOL
    ).astype(jnp.bfloat16)
    attended = out_tiles[0]
    grad_query = query_tiles[0]
    return (attended, grad_query, grad_key, grad_value, own_coarse_keys, own_coarse_values)


SLOTS = 2
CORES_HERE = CORES * PAIR


def remote(src, dst, sent, got, target):
    return pltpu.make_async_remote_copy(
        src_ref=src,
        dst_ref=dst,
        send_sem=sent,
        recv_sem=got,
        device_id={"ctx": target},
        device_id_type=pl.DeviceIdType.MESH,
    )


def wait_for(ref, semaphore):
    pltpu.make_async_copy(ref, ref, semaphore).wait()


def block(index, size):
    return pl.ds(pl.multiple_of(index * size, size), size)


def meet(devices, me):
    barrier = pltpu.get_barrier_semaphore()
    for k in range(1, devices):
        pl.semaphore_signal(
            barrier,
            inc=1,
            device_id={"ctx": lax.rem(me + k, devices)},
            device_id_type=pl.DeviceIdType.MESH,
        )
    pl.semaphore_wait(barrier, devices - 1)


def fused_kernel(devices, place_ref, spot, k_ref, v_ref, q_ref, g_ref,
                 ro_ref, rq_ref, rk_ref, rv_ref, rc_ref,
                 keys_in, values_in, queries, grads, out_o, out_q, out_k, out_v, out_c,
                 joined, joined_pool, keys_t, keys_pool, values_t, values_pool, pairs, kept,
                 kept_pool, total,
                 send_in, kv_sem, own_sem, q_sem, g_sem, send_out, back_sem, own_out):
    me = lax.axis_index("ctx")
    levels = devices // CORES_HERE
    per_level = HEADS // levels
    tokens = devices * TILE
    pools = tokens // POOL
    per_tile = TILE // POOL
    listed_rows = SEL * TILE
    level = me // CORES_HERE
    upper = level // 2
    near = (1 - upper) * level + upper * (levels - 1 - level)
    extra_at = CORES * (level % PAIR) + CORES - 1
    two = me % CORES_HERE == extra_at
    apart = me % CORES_HERE - extra_at
    count = 1 + (CORES_HERE * CORES_HERE - apart * apart) // (CORES_HERE * CORES_HERE)
    scaling = HEAD_DIM ** (-0.5)
    rate = scaling * math.log2(math.e)

    def level_at(step):
        turn = step + near * (1 - step // 2) * (1 - 2 * step)
        return (1 - upper) * turn + upper * (levels - 1 - turn)

    meet(devices, me)

    my_rows = block(me, TILE)

    def send_pair(index):
        def step(i, carry):
            goal = level_at(i // per_level)
            j = lax.rem(i + me, per_level)
            spare = j // CORES_HERE
            owner = (
                goal * CORES_HERE
                + (1 - spare) * j
                + spare * (CORES * (goal % PAIR) + CORES - 1)
            )
            columns = block(goal * per_level + j, HEAD_DIM)
            if index == 0:
                moves = [
                    (k_ref, keys_in.at[spare, my_rows, :], kv_sem.at[0, spare]),
                    (v_ref, values_in.at[spare, my_rows, :], kv_sem.at[1, spare]),
                ]
            else:
                moves = [
                    (q_ref, queries.at[spare, my_rows, :], q_sem.at[spare, me]),
                    (g_ref, grads.at[spare, my_rows, :], g_sem.at[spare, me]),
                ]

            @pl.when(owner != me)
            def _():
                for n, (src, dst, got) in enumerate(moves):
                    remote(src.at[:, columns], dst, send_in.at[2 * index + n], got, owner).start()

            @pl.when(owner == me)
            def _():
                for n, (src, dst, got) in enumerate(moves):
                    arrived = own_sem.at[n, spare] if index == 0 else got
                    pltpu.make_async_copy(src.at[:, columns], dst, arrived).start()

            return carry

        lax.fori_loop(0, HEADS, step, 0)

    send_pair(0)
    send_pair(1)

    for i in range(CORES_HERE):
        kept[i, SEL] = jnp.zeros((TILE, 2 * HEAD_DIM), jnp.bfloat16)
    out_c[...] = jnp.zeros_like(out_c)

    def send_back(slot, tile, moves):
        @pl.when(tile != me)
        def _():
            for a, src, dst in moves:
                remote(src, dst, send_out.at[a, slot], back_sem.at[a], tile).start()

        @pl.when(tile == me)
        def _():
            for a, src, dst in moves:
                pltpu.make_async_copy(src, dst, own_out.at[a, slot]).start()

    def run_head(slot, carry):
        head = level * per_level + (1 - slot) * (me % CORES_HERE) + slot * CORES_HERE
        columns = block(head, HEAD_DIM)

        def send_rows(tile):
            rows = block(tile, TILE)
            send_back(
                slot,
                tile,
                [
                    (0, out_o.at[slot, rows, :], ro_ref.at[:, columns]),
                    (1, out_q.at[slot, rows, :], rq_ref.at[:, columns]),
                ],
            )

        for n, (source, turned, turned_pool) in enumerate(
            ((keys_in, keys_t, keys_pool), (values_in, values_t, values_pool))
        ):
            wait_for(source.at[slot, pl.ds(0, tokens - TILE), :], kv_sem.at[n, slot])
            wait_for(source.at[slot, my_rows, :], own_sem.at[n, slot])
            part = slice(n * HEAD_DIM, (n + 1) * HEAD_DIM)
            rows = source[slot]
            means = jnp.sum(rows.astype(jnp.float32).reshape(pools, POOL, HEAD_DIM), axis=1)
            means = (means * (1.0 / POOL)).astype(jnp.bfloat16)
            joined_pool[:, part] = means
            turned_pool[...] = means.T
            for tile in range(devices):
                one = rows[tile * TILE : (tile + 1) * TILE]
                joined[tile, :, part] = one
                turned[tile] = one.T
        total[...] = jnp.zeros_like(total)

        def tile_step(n, carry):
            i = lax.rem(n, CORES_HERE)
            t = level_at(n // CORES_HERE) * CORES_HERE + i
            rows = block(t, TILE)

            @pl.when(n > 0)
            def _():
                before = n - 1
                send_rows(
                    level_at(before // CORES_HERE) * CORES_HERE + lax.rem(before, CORES_HERE)
                )

            wait_for(queries.at[slot, rows, :], q_sem.at[slot, t])
            wait_for(grads.at[slot, rows, :], g_sem.at[slot, t])
            query = queries[slot, rows, :]
            grad = grads[slot, rows, :]
            blank = jnp.zeros_like(query)
            paired = jnp.concatenate(
                [
                    jnp.concatenate([query, blank], axis=1),
                    jnp.concatenate([blank, grad], axis=1),
                ],
                axis=0,
            )
            pairs[i] = paired
            places = [place_ref[t, j] for j in range(SEL)]
            listed = jnp.concatenate(
                [joined[place] for place in places] + [joined_pool[...]], axis=0
            )
            both = contract(listed, paired, 1, 1)
            scores = both[:, :TILE]
            prob_grad = both[:, TILE:]
            summit = jnp.max(scores, axis=0, keepdims=True)
            raised = jnp.exp2((scores - summit) * rate)
            scale = 1.0 / jnp.sum(raised, axis=0, keepdims=True)
            dots = jnp.sum(raised * prob_grad, axis=0, keepdims=True) * scale
            weights = raised * scale
            score_grad = (weights * (prob_grad - dots)).astype(jnp.bfloat16)
            rounded = weights.astype(jnp.bfloat16)
            for part, values in ((0, score_grad), (HEAD_DIM, rounded)):
                for j in range(SEL):
                    kept[i, j, :, part : part + HEAD_DIM] = values[j * TILE : (j + 1) * TILE]
                kept_pool[i, :, part : part + HEAD_DIM] = values[listed_rows:]
            listed_kt = jnp.concatenate(
                [keys_t[place] for place in places] + [keys_pool[...]], axis=1
            )
            listed_vt = jnp.concatenate(
                [values_t[place] for place in places] + [values_pool[...]], axis=1
            )
            out_t = jnp.dot(listed_vt, rounded, preferred_element_type=jnp.float32)
            dq_t = jnp.dot(listed_kt, score_grad, preferred_element_type=jnp.float32) * scaling
            out_o[slot, rows, :] = out_t.T.astype(jnp.bfloat16)
            out_q[slot, rows, :] = dq_t.T.astype(jnp.bfloat16)
            return carry

        def add_terms(g, carry):
            first = level_at(g) * CORES_HERE
            facing = pairs[...].reshape(CORES_HERE * 2 * TILE, 2 * HEAD_DIM)
            for u in range(devices):
                found = jnp.concatenate(
                    [kept[i, spot[first + i, u]] for i in range(CORES_HERE)],
                    axis=1,
                )
                total[u * TILE : (u + 1) * TILE, :] += jnp.dot(
                    found, facing, preferred_element_type=jnp.float32
                )
            found = jnp.concatenate([kept_pool[i] for i in range(CORES_HERE)], axis=1)
            total[tokens:, :] += jnp.dot(found, facing, preferred_element_type=jnp.float32)
            return carry

        def group_step(g, carry):
            lax.fori_loop(g * CORES_HERE, (g + 1) * CORES_HERE, tile_step, 0)
            return add_terms(g, carry)

        lax.fori_loop(0, levels, group_step, 0)
        send_rows(level_at(levels - 1) * CORES_HERE + CORES_HERE - 1)
        for ref, at, factor in ((out_k, 0, scaling), (out_v, HEAD_DIM, 1.0)):
            coarse = total[tokens:, at : at + HEAD_DIM] * factor
            fine = total[:tokens, at : at + HEAD_DIM] * factor
            fine = fine.reshape(pools, POOL, HEAD_DIM) + (coarse * (1.0 / POOL))[:, None, :]
            ref[slot] = fine.reshape(tokens, HEAD_DIM).astype(jnp.bfloat16)
            start = 0 if at == 0 else per_tile
            for tile in range(devices):
                out_c[slot, tile, start : start + per_tile, :] = coarse[
                    tile * per_tile : (tile + 1) * per_tile
                ]

        def send_sums(n, carry):
            tile = level_at(n // CORES_HERE) * CORES_HERE + lax.rem(n, CORES_HERE)
            rows = block(tile, TILE)
            send_back(
                slot,
                tile,
                [
                    (2, out_k.at[slot, rows, :], rk_ref.at[:, columns]),
                    (3, out_v.at[slot, rows, :], rv_ref.at[:, columns]),
                    (4, out_c.at[slot, tile], rc_ref.at[head]),
                ],
            )
            return carry

        lax.fori_loop(0, devices, send_sums, 0)
        return carry

    lax.fori_loop(0, count, run_head, 0)

    stores = (out_o, out_q, out_k, out_v)
    landed = (ro_ref, rq_ref, rk_ref, rv_ref)

    def sent(slot):
        for a, ref in enumerate(stores):
            wait_for(ref.at[slot, pl.ds(0, tokens - TILE), :], send_out.at[a, slot])
            wait_for(ref.at[slot, my_rows, :], own_out.at[a, slot])
        wait_for(out_c.at[slot, pl.ds(0, devices - 1)], send_out.at[4, slot])
        wait_for(out_c.at[slot, me], own_out.at[4, slot])

    def finish(own):
        for n, ref in enumerate((k_ref, v_ref, q_ref, g_ref)):
            wait_for(ref.at[:, pl.ds(0, (HEADS - own) * HEAD_DIM)], send_in.at[n])
        for a, ref in enumerate(landed):
            wait_for(ref.at[:, pl.ds(0, (HEADS - own) * HEAD_DIM)], back_sem.at[a])
        wait_for(rc_ref.at[pl.ds(0, HEADS - own)], back_sem.at[4])

    sent(0)

    @pl.when(two)
    def _():
        sent(1)
        finish(2)

    @pl.when(jnp.logical_not(two))
    def _():
        finish(1)


def spots(selected):
    listed = selected[:, :, None] == jnp.arange(selected.shape[0], dtype=jnp.int32)
    shift = jnp.arange(SEL, dtype=jnp.int32)[None, :, None] - SEL
    return SEL + jnp.sum(jnp.where(listed, shift, 0), axis=1, dtype=jnp.int32)


def fused(selected, arrays, devices):
    tokens = devices * TILE
    pools = tokens // POOL
    flat = jax.ShapeDtypeStruct((TILE, HEADS * HEAD_DIM), jnp.bfloat16)
    coarse = jax.ShapeDtypeStruct((HEADS, 8, HEAD_DIM), jnp.float32)
    slabs = pltpu.VMEM((SLOTS, tokens, HEAD_DIM), jnp.bfloat16)
    turned = pltpu.VMEM((devices, HEAD_DIM, TILE), jnp.bfloat16)
    turned_pool = pltpu.VMEM((HEAD_DIM, pools), jnp.bfloat16)
    return pl.pallas_call(
        functools.partial(fused_kernel, devices),
        out_shape=[flat] * 4 + [coarse],
        in_specs=[pl.BlockSpec(memory_space=pltpu.SMEM)] * 2 + [pl.BlockSpec(memory_space=pl.ANY)] * 4,
        out_specs=[pl.BlockSpec(memory_space=pl.ANY)] * 5,
        scratch_shapes=[
            slabs,
            slabs,
            slabs,
            slabs,
            slabs,
            slabs,
            slabs,
            slabs,
            pltpu.VMEM((SLOTS, devices, 8, HEAD_DIM), jnp.float32),
            pltpu.VMEM((devices, TILE, 2 * HEAD_DIM), jnp.bfloat16),
            pltpu.VMEM((pools, 2 * HEAD_DIM), jnp.bfloat16),
            turned,
            turned_pool,
            turned,
            turned_pool,
            pltpu.VMEM((CORES_HERE, 2 * TILE, 2 * HEAD_DIM), jnp.bfloat16),
            pltpu.VMEM((CORES_HERE, SEL + 1, TILE, 2 * HEAD_DIM), jnp.bfloat16),
            pltpu.VMEM((CORES_HERE, pools, 2 * HEAD_DIM), jnp.bfloat16),
            pltpu.VMEM((tokens + pools, 2 * HEAD_DIM), jnp.float32),
            pltpu.SemaphoreType.DMA((4,)),
            pltpu.SemaphoreType.DMA((2, SLOTS)),
            pltpu.SemaphoreType.DMA((2, SLOTS)),
            pltpu.SemaphoreType.DMA((SLOTS, devices)),
            pltpu.SemaphoreType.DMA((SLOTS, devices)),
            pltpu.SemaphoreType.DMA((5, SLOTS)),
            pltpu.SemaphoreType.DMA((5,)),
            pltpu.SemaphoreType.DMA((5, SLOTS)),
        ],
        compiler_params=pltpu.CompilerParams(collective_id=0, has_side_effects=True),
        name="exchange_heads",
    )(selected, spots(selected), *arrays)


def exchange_shards(query_rows, key_rows, value_rows, out_grad, selected):
    devices = lax.axis_size("ctx")
    out, dq, dk, dv, coarse = fused(
        selected, (key_rows, value_rows, query_rows, out_grad), devices
    )
    per_tile = TILE // POOL
    flat = lambda part: part.transpose(1, 0, 2).reshape(per_tile, HEADS * HEAD_DIM)
    return (
        out,
        dq,
        dk,
        dv,
        flat(coarse[:, :per_tile]),
        flat(coarse[:, per_tile : 2 * per_tile]),
    )


def shards(query_rows, key_rows, value_rows, out_grad, selected):
    devices = lax.axis_size("ctx")
    fits = devices == 4 * CORES * PAIR and query_rows.shape[0] == TILE
    chosen = exchange_shards if fits else listed_shards
    return chosen(query_rows, key_rows, value_rows, out_grad, selected)


def solution(mesh):
    in_specs = (
        P(("groups", "ctx"), None),
        P(("groups", "ctx"), None),
        P(("groups", "ctx"), None),
        P(("groups", "ctx"), None),
        P("groups", None),
    )
    out_specs = (
        P(("groups", "ctx"), None),
        P(("groups", "ctx"), None),
        P(("groups", "ctx"), None),
        P(("groups", "ctx"), None),
        P(("groups", "ctx"), None),
        P(("groups", "ctx"), None),
    )
    return jax.shard_map(shards, mesh=mesh, in_specs=in_specs, out_specs=out_specs, check_vma=False)
```

time: 182 us -> 134 us (0.74)
  the two profiles are of different devices: /device:TPU:11 before, /device:TPU:3 now
where the time goes in v1:
time: 134 us
  Pallas kernels  124 us (93%)
  local copies, waits for them, and re-layouts  8.35 us (6%)
    pallas_call x1, Pallas kernels, fused(): pl.pallas_call(functools.partial(fused_kernel, devices), out_shape=[flat]...  124 us
    unnamed x13, local copies, waits for them, and re-layouts  6.76 us

profile of v1, /device:TPU:3, one launch (start us, length us, event | category | flops | bytes accessed | tf_op | source)
XLA Modules:
  0.0 134.0 jit_solution(18350024315729984275)
XLA Ops:
  0.6 0.8 copy.14.place_ref
  1.4 0.0 copy-start.3
  1.4 0.1 select_reduce_fusion
  1.5 0.5 copy-done.3
  2.0 0.6 broadcast_add_fusion.spot
  2.6 124.3 %exchange_heads.1 = (bf16[128,2560]{1,0:T(8,128)(2,1)}, bf16[128,2560]{1,0:T(8,128)(2,1)}, bf16[128,2560]{1,0:T(8,128)(2,1)}, bf16[128,2560]{1,0:T(8,128)(2,1)}, f32[20,8,128]{2,1,0:T(8,128)}) custom-call(s32[16,8]{1,0:T(8,128)} %copy-done.3, s32[16,16]{1,0:T(8,128)} %broadcast_add_fusion.spot, bf16[128,2560]{1,0:T(8,128)(2,1)} %k_ref.1, ...), custom_call_target="tpu_custom_call" | custom-call | tf_op jit(solution)/shard_map/exchange_heads/pallas_call | solution.py:471
  126.9 1.6 %slice_bitcast_fusion = (f32[2,2560]{1,0:T(2,128)}, f32[2,2560]{1,0:T(2,128)}) fusion(f32[20,8,128]{2,1,0:T(8,128)} %get-tuple-element.15), kind=kLoop, calls=%fused_computation.2 | loop fusion | bytes 81920 | tf_op jit(solution)/shard_map/reshape | solution.py:516
  128.4 0.0 copy-start.2
  128.4 2.0 %copy.19 = bf16[128,2560]{1,0:T(8,128)(2,1)} copy(bf16[128,2560]{1,0:T(8,128)(2,1)} %get-tuple-element.24) | data formatting | bytes 1310720
  130.5 0.0 copy-done.2
  130.5 0.0 copy-start.1
  130.5 0.8 copy.20
  131.3 0.5 copy-done.1
  131.8 0.0 copy-start
  131.8 0.8 copy.21
  132.6 0.5 copy-done
  133.1 0.8 copy.22
  (1 shorter events, 0.0 us)
Async XLA Ops:
  1.4 0.6 copy-start.3
  128.4 2.0 %copy-start.2 = (bf16[128,2560]{1,0:T(8,128)(2,1)S(1)}, bf16[128,2560]{1,0:T(8,128)(2,1)}, u32[]{:S(2)}) copy-start(bf16[128,2560]{1,0:T(8,128)(2,1)} %get-tuple-element.25) | copy-start | bytes 1966084
  130.5 1.3 copy-start.1
  131.8 1.3 copy-start

commit v2 on v1

--- a/solution.py
+++ b/solution.py
@@ -201,11 +201,11 @@
     pl.semaphore_wait(barrier, devices - 1)
 
 
-def fused_kernel(devices, place_ref, spot, k_ref, v_ref, q_ref, g_ref,
+def fused_kernel(devices, chosen_ref, k_ref, v_ref, q_ref, g_ref,
                  ro_ref, rq_ref, rk_ref, rv_ref, rc_ref,
                  keys_in, values_in, queries, grads, out_o, out_q, out_k, out_v, out_c,
                  joined, joined_pool, keys_t, keys_pool, values_t, values_pool, pairs, kept,
-                 kept_pool, total,
+                 kept_pool, total, place_ref, spot, chosen_sem,
                  send_in, kv_sem, own_sem, q_sem, g_sem, send_out, back_sem, own_out):
     me = lax.axis_index("ctx")
     levels = devices // CORES_HERE
@@ -269,12 +269,24 @@
 
         lax.fori_loop(0, HEADS, step, 0)
 
+    chosen = pltpu.make_async_copy(chosen_ref, place_ref, chosen_sem)
+    chosen.start()
     send_pair(0)
     send_pair(1)
+    chosen.wait()
+
+    def find(t, carry):
+        for u in range(devices):
+            at = SEL
+            for j in range(SEL):
+                at = jnp.where(place_ref[j, t] == u, j, at)
+            spot[t, u] = at
+        return carry
+
+    lax.fori_loop(0, devices, find, 0)
 
     for i in range(CORES_HERE):
         kept[i, SEL] = jnp.zeros((TILE, 2 * HEAD_DIM), jnp.bfloat16)
-    out_c[...] = jnp.zeros_like(out_c)
 
     def send_back(slot, tile, moves):
         @pl.when(tile != me)
@@ -344,7 +356,7 @@
                 axis=0,
             )
             pairs[i] = paired
-            places = [place_ref[t, j] for j in range(SEL)]
+            places = [place_ref[j, t] for j in range(SEL)]
             listed = jnp.concatenate(
                 [joined[place] for place in places] + [joined_pool[...]], axis=0
             )
@@ -454,24 +466,19 @@
         finish(1)
 
 
-def spots(selected):
-    listed = selected[:, :, None] == jnp.arange(selected.shape[0], dtype=jnp.int32)
-    shift = jnp.arange(SEL, dtype=jnp.int32)[None, :, None] - SEL
-    return SEL + jnp.sum(jnp.where(listed, shift, 0), axis=1, dtype=jnp.int32)
-
-
 def fused(selected, arrays, devices):
+    turned_list = selected.T
     tokens = devices * TILE
     pools = tokens // POOL
     flat = jax.ShapeDtypeStruct((TILE, HEADS * HEAD_DIM), jnp.bfloat16)
-    coarse = jax.ShapeDtypeStruct((HEADS, 8, HEAD_DIM), jnp.float32)
+    coarse = jax.ShapeDtypeStruct((HEADS, 2 * TILE // POOL, HEAD_DIM), jnp.float32)
     slabs = pltpu.VMEM((SLOTS, tokens, HEAD_DIM), jnp.bfloat16)
     turned = pltpu.VMEM((devices, HEAD_DIM, TILE), jnp.bfloat16)
     turned_pool = pltpu.VMEM((HEAD_DIM, pools), jnp.bfloat16)
     return pl.pallas_call(
         functools.partial(fused_kernel, devices),
         out_shape=[flat] * 4 + [coarse],
-        in_specs=[pl.BlockSpec(memory_space=pltpu.SMEM)] * 2 + [pl.BlockSpec(memory_space=pl.ANY)] * 4,
+        in_specs=[pl.BlockSpec(memory_space=pl.ANY)] * 5,
         out_specs=[pl.BlockSpec(memory_space=pl.ANY)] * 5,
         scratch_shapes=[
             slabs,
@@ -482,7 +489,7 @@
             slabs,
             slabs,
             slabs,
-            pltpu.VMEM((SLOTS, devices, 8, HEAD_DIM), jnp.float32),
+            pltpu.VMEM((SLOTS, devices, 2 * TILE // POOL, HEAD_DIM), jnp.float32),
             pltpu.VMEM((devices, TILE, 2 * HEAD_DIM), jnp.bfloat16),
             pltpu.VMEM((pools, 2 * HEAD_DIM), jnp.bfloat16),
             turned,
@@ -493,6 +500,9 @@
             pltpu.VMEM((CORES_HERE, SEL + 1, TILE, 2 * HEAD_DIM), jnp.bfloat16),
             pltpu.VMEM((CORES_HERE, pools, 2 * HEAD_DIM), jnp.bfloat16),
             pltpu.VMEM((tokens + pools, 2 * HEAD_DIM), jnp.float32),
+            pltpu.SMEM(turned_list.shape, jnp.int32),
+            pltpu.SMEM((devices, devices), jnp.int32),
+            pltpu.SemaphoreType.DMA,
             pltpu.SemaphoreType.DMA((4,)),
             pltpu.SemaphoreType.DMA((2, SLOTS)),
             pltpu.SemaphoreType.DMA((2, SLOTS)),
@@ -504,24 +514,61 @@
         ],
         compiler_params=pltpu.CompilerParams(collective_id=0, has_side_effects=True),
         name="exchange_heads",
-    )(selected, spots(selected), *arrays)
+    )(turned_list, *arrays)
+
+
+def place_kernel(pieces, a_ref, b_ref, c_ref, d_ref, coarse_ref,
+                 oa_ref, ob_ref, oc_ref, od_ref, keys_ref, values_ref, held, in_sem, out_sem):
+    sources = (a_ref, b_ref, c_ref, d_ref)
+    targets = (oa_ref, ob_ref, oc_ref, od_ref)
+    height = a_ref.shape[0] // pieces
+    steps = [(n, p) for p in range(pieces) for n in range(4)]
+
+    def move(n, p, out):
+        rows = pl.ds(p * height, height)
+        here = held.at[n, rows, :]
+        if out:
+            return pltpu.make_async_copy(here, targets[n].at[rows, :], out_sem.at[n, p])
+        return pltpu.make_async_copy(sources[n].at[rows, :], here, in_sem.at[n, p])
+
+    for n, p in steps:
+        move(n, p, False).start()
+    per_tile = TILE // POOL
+    for head in range(HEADS):
+        columns = slice(head * HEAD_DIM, (head + 1) * HEAD_DIM)
+        keys_ref[:, columns] = coarse_ref[head, :per_tile]
+        values_ref[:, columns] = coarse_ref[head, per_tile:]
+    for n, p in steps:
+        move(n, p, False).wait()
+        move(n, p, True).start()
+    for n, p in steps:
+        move(n, p, True).wait()
+
+
+def place(parts, coarse):
+    pieces = 2
+    shape = jax.ShapeDtypeStruct(parts[0].shape, jnp.bfloat16)
+    sums = jax.ShapeDtypeStruct((TILE // POOL, HEADS * HEAD_DIM), jnp.float32)
+    anywhere = [pl.BlockSpec(memory_space=pl.ANY)] * 4
+    whole = pl.BlockSpec(memory_space=pltpu.VMEM)
+    return pl.pallas_call(
+        functools.partial(place_kernel, pieces),
+        out_shape=[shape] * 4 + [sums] * 2,
+        in_specs=anywhere + [whole],
+        out_specs=anywhere + [whole] * 2,
+        scratch_shapes=[
+            pltpu.VMEM((4, *shape.shape), jnp.bfloat16),
+            pltpu.SemaphoreType.DMA((4, pieces)),
+            pltpu.SemaphoreType.DMA((4, pieces)),
+        ],
+        name="place",
+    )(*parts, coarse)
 
 
 def exchange_shards(query_rows, key_rows, value_rows, out_grad, selected):
     devices = lax.axis_size("ctx")
-    out, dq, dk, dv, coarse = fused(
-        selected, (key_rows, value_rows, query_rows, out_grad), devices
-    )
-    per_tile = TILE // POOL
-    flat = lambda part: part.transpose(1, 0, 2).reshape(per_tile, HEADS * HEAD_DIM)
-    return (
-        out,
-        dq,
-        dk,
-        dv,
-        flat(coarse[:, :per_tile]),
-        flat(coarse[:, per_tile : 2 * per_tile]),
-    )
+    *parts, coarse = fused(selected, (key_rows, value_rows, query_rows, out_grad), devices)
+    return tuple(place(parts, coarse))
 
 
 def shards(query_rows, key_rows, value_rows, out_grad, selected):

time: 134 us -> 128 us (0.955)
  local copies, waits for them, and re-layouts: 8.35 us -> 0 us
  Pallas kernels: 124 us -> 127 us
    unnamed x13 -> x0, local copies, waits for them, and re-layouts: 6.76 us -> none
    pallas_call x0 -> x1, Pallas kernels: none -> 3.98 us  [place(): pl.pallas_call(functools.partial(place_kernel, pieces), out_shape=[shape]...]
    reshape x1 -> x0, local copies, waits for them, and re-layouts: 1.59 us -> none  [exchange_shards(): part.transpose(1, 0, 2).reshape(per_tile, HEADS * HEAD_DIM)]
    pallas_call x1, Pallas kernels: 124 us -> 123 us  [fused(): pl.pallas_call(functools.partial(fused_kernel, devices), out_shape=[flat]...]
where the time goes in v2:
time: 128 us
  Pallas kernels  127 us (99%)
    pallas_call x1, Pallas kernels, fused(): pl.pallas_call(functools.partial(fused_kernel, devices), out_shape=[flat]...  123 us
    pallas_call x1, Pallas kernels, place(): pl.pallas_call(functools.partial(place_kernel, pieces), out_shape=[shape]...  3.98 us

profile of v2, /device:TPU:3, one launch (start us, length us, event | category | flops | bytes accessed | tf_op | source)
XLA Modules:
  0.0 127.5 jit_solution(11092184828430501919)
XLA Ops:
  0.6 122.9 %exchange_heads.1 = (bf16[128,2560]{1,0:T(8,128)(2,1)}, bf16[128,2560]{1,0:T(8,128)(2,1)}, bf16[128,2560]{1,0:T(8,128)(2,1)}, bf16[128,2560]{1,0:T(8,128)(2,1)}, f32[20,4,128]{2,1,0:T(4,128)}) custom-call(s32[8,16]{1,0:T(8,128)} %bitcast.1, bf16[128,2560]{1,0:T(8,128)(2,1)} %k_ref.1, bf16[128,2560]{1,0:T(8,128)(2,1)} %v_ref.1, bf16[128,2560]{1,0:T(8,128)(2,1)} %q_ref.1, ...), custom_call_target="tpu_custom_call" | custom-call | tf_op jit(solution)/shard_map/exchange_heads/pallas_call | solution.py:478
  123.6 4.0 %place.1 = (bf16[128,2560]{1,0:T(8,128)(2,1)}, bf16[128,2560]{1,0:T(8,128)(2,1)}, bf16[128,2560]{1,0:T(8,128)(2,1)}, bf16[128,2560]{1,0:T(8,128)(2,1)}, f32[2,2560]{1,0:T(2,128)}, /*index=5*/f32[2,2560]{1,0:T(2,128)}) custom-call(bf16[128,2560]{1,0:T(8,128)(2,1)} %get-tuple-element.11.a_ref, bf16[128,2560]{1,0:T(8,128)(2,1)} %get-tuple-element.12.b_ref, ...), custom_call_target="tpu_custom_call" | custom-call | tf_op jit(solution)/shard_map/place/pallas_call | solution.py:554

commit v3 on v2

--- a/solution.py
+++ b/solution.py
@@ -467,10 +467,12 @@
 
 
 def fused(selected, arrays, devices):
-    turned_list = selected.T
+    turned_list, *arrays = (
+        pltpu.with_memory_space_constraint(part, pltpu.HBM) for part in (selected.T, *arrays)
+    )
     tokens = devices * TILE
     pools = tokens // POOL
-    flat = jax.ShapeDtypeStruct((TILE, HEADS * HEAD_DIM), jnp.bfloat16)
+    flat = pltpu.VMEM((TILE, HEADS * HEAD_DIM), jnp.bfloat16)
     coarse = jax.ShapeDtypeStruct((HEADS, 2 * TILE // POOL, HEAD_DIM), jnp.float32)
     slabs = pltpu.VMEM((SLOTS, tokens, HEAD_DIM), jnp.bfloat16)
     turned = pltpu.VMEM((devices, HEAD_DIM, TILE), jnp.bfloat16)
@@ -478,8 +480,9 @@
     return pl.pallas_call(
         functools.partial(fused_kernel, devices),
         out_shape=[flat] * 4 + [coarse],
-        in_specs=[pl.BlockSpec(memory_space=pl.ANY)] * 5,
-        out_specs=[pl.BlockSpec(memory_space=pl.ANY)] * 5,
+        in_specs=[pl.BlockSpec(memory_space=pltpu.HBM)] * 5,
+        out_specs=[pl.BlockSpec(memory_space=pltpu.VMEM)] * 4
+        + [pl.BlockSpec(memory_space=pl.ANY)],
         scratch_shapes=[
             slabs,
             slabs,
@@ -512,55 +515,44 @@
             pltpu.SemaphoreType.DMA((5,)),
             pltpu.SemaphoreType.DMA((5, SLOTS)),
         ],
-        compiler_params=pltpu.CompilerParams(collective_id=0, has_side_effects=True),
+        compiler_params=pltpu.CompilerParams(
+            collective_id=0, has_side_effects=True, vmem_limit_bytes=40 * 2**20
+        ),
         name="exchange_heads",
     )(turned_list, *arrays)
 
 
-def place_kernel(pieces, a_ref, b_ref, c_ref, d_ref, coarse_ref,
-                 oa_ref, ob_ref, oc_ref, od_ref, keys_ref, values_ref, held, in_sem, out_sem):
-    sources = (a_ref, b_ref, c_ref, d_ref)
-    targets = (oa_ref, ob_ref, oc_ref, od_ref)
-    height = a_ref.shape[0] // pieces
-    steps = [(n, p) for p in range(pieces) for n in range(4)]
-
-    def move(n, p, out):
-        rows = pl.ds(p * height, height)
-        here = held.at[n, rows, :]
-        if out:
-            return pltpu.make_async_copy(here, targets[n].at[rows, :], out_sem.at[n, p])
-        return pltpu.make_async_copy(sources[n].at[rows, :], here, in_sem.at[n, p])
-
-    for n, p in steps:
-        move(n, p, False).start()
+def place_kernel(a_ref, b_ref, c_ref, d_ref, coarse_ref,
+                 oa_ref, ob_ref, oc_ref, od_ref, keys_ref, values_ref, sem):
+    moves = [
+        pltpu.make_async_copy(source, target, sem.at[n])
+        for n, (source, target) in enumerate(
+            zip((a_ref, b_ref, c_ref, d_ref), (oa_ref, ob_ref, oc_ref, od_ref))
+        )
+    ]
+    for move in moves:
+        move.start()
     per_tile = TILE // POOL
     for head in range(HEADS):
         columns = slice(head * HEAD_DIM, (head + 1) * HEAD_DIM)
         keys_ref[:, columns] = coarse_ref[head, :per_tile]
         values_ref[:, columns] = coarse_ref[head, per_tile:]
-    for n, p in steps:
-        move(n, p, False).wait()
-        move(n, p, True).start()
-    for n, p in steps:
-        move(n, p, True).wait()
+    for move in moves:
+        move.wait()
 
 
 def place(parts, coarse):
-    pieces = 2
     shape = jax.ShapeDtypeStruct(parts[0].shape, jnp.bfloat16)
     sums = jax.ShapeDtypeStruct((TILE // POOL, HEADS * HEAD_DIM), jnp.float32)
-    anywhere = [pl.BlockSpec(memory_space=pl.ANY)] * 4
     whole = pl.BlockSpec(memory_space=pltpu.VMEM)
+    parts = [pltpu.with_memory_space_constraint(part, pltpu.VMEM) for part in parts]
     return pl.pallas_call(
-        functools.partial(place_kernel, pieces),
+        place_kernel,
         out_shape=[shape] * 4 + [sums] * 2,
-        in_specs=anywhere + [whole],
-        out_specs=anywhere + [whole] * 2,
-        scratch_shapes=[
-            pltpu.VMEM((4, *shape.shape), jnp.bfloat16),
-            pltpu.SemaphoreType.DMA((4, pieces)),
-            pltpu.SemaphoreType.DMA((4, pieces)),
-        ],
+        in_specs=[whole] * 5,
+        out_specs=[pl.BlockSpec(memory_space=pl.ANY)] * 4 + [whole] * 2,
+        scratch_shapes=[pltpu.SemaphoreType.DMA((4,))],
+        compiler_params=pltpu.CompilerParams(vmem_limit_bytes=2**23),
         name="place",
     )(*parts, coarse)
 

time: 128 us -> 126 us (0.984)
  Pallas kernels: 127 us -> 125 us
    pallas_call x1, Pallas kernels: 3.98 us -> 2.13 us  [place(): pl.pallas_call(place_kernel, out_shape=[shape] * 4 + [sums] * 2, in_specs...]
where the time goes in v3:
time: 126 us; the launch traced here: 125 us
  Pallas kernels  125 us (99%)
    pallas_call x1, Pallas kernels, fused(): pl.pallas_call(functools.partial(fused_kernel, devices), out_shape=[flat]...  123 us

profile of v3, /device:TPU:3, one launch (start us, length us, event | category | flops | bytes accessed | tf_op | source)
XLA Modules:
  0.0 125.5 jit_solution(7398421430087066973)
XLA Ops:
  0.6 122.7 %exchange_heads.1 = (bf16[128,2560]{1,0:T(8,128)(2,1)S(1)}, bf16[128,2560]{1,0:T(8,128)(2,1)S(1)}, bf16[128,2560]{1,0:T(8,128)(2,1)S(1)}, bf16[128,2560]{1,0:T(8,128)(2,1)S(1)}, f32[20,4,128]{2,1,0:T(4,128)S(1)}) custom-call(s32[8,16]{1,0:T(8,128)} %bitcast.1, bf16[128,2560]{1,0:T(8,128)(2,1)} %k_ref.1, bf16[128,2560]{1,0:T(8,128)(2,1)} %v_ref.1, ...), custom_call_target="tpu_custom_call" | custom-call | tf_op jit(solution)/shard_map/exchange_heads/pallas_call | solution.py:480
  123.4 2.1 %place.1 = (bf16[128,2560]{1,0:T(8,128)(2,1)}, bf16[128,2560]{1,0:T(8,128)(2,1)}, bf16[128,2560]{1,0:T(8,128)(2,1)}, bf16[128,2560]{1,0:T(8,128)(2,1)}, f32[2,2560]{1,0:T(2,128)}, /*index=5*/f32[2,2560]{1,0:T(2,128)}) custom-call(bf16[128,2560]{1,0:T(8,128)(2,1)S(1)} %get-tuple-element.11.a_ref, bf16[128,2560]{1,0:T(8,128)(2,1)S(1)} %get-tuple-element.12.b_ref, ...), custom_call_target="tpu_custom_call" | custom-call | tf_op jit(solution)/shard_map/place/pallas_call | solution.py:549

commit v4 on v3

--- a/solution.py
+++ b/solution.py
@@ -189,16 +189,13 @@
     return pl.ds(pl.multiple_of(index * size, size), size)
 
 
-def meet(devices, me):
-    barrier = pltpu.get_barrier_semaphore()
-    for k in range(1, devices):
-        pl.semaphore_signal(
-            barrier,
-            inc=1,
-            device_id={"ctx": lax.rem(me + k, devices)},
-            device_id_type=pl.DeviceIdType.MESH,
-        )
-    pl.semaphore_wait(barrier, devices - 1)
+def greet(target):
+    pl.semaphore_signal(
+        pltpu.get_barrier_semaphore(),
+        inc=1,
+        device_id={"ctx": target},
+        device_id_type=pl.DeviceIdType.MESH,
+    )
 
 
 def fused_kernel(devices, chosen_ref, k_ref, v_ref, q_ref, g_ref,
@@ -225,14 +222,34 @@
     rate = scaling * math.log2(math.e)
 
     def level_at(step):
-        turn = step + near * (1 - step // 2) * (1 - 2 * step)
+        turn = step + near * (1 - 3 * (step // 2) + 2 * (step // 3))
         return (1 - upper) * turn + upper * (levels - 1 - turn)
 
-    meet(devices, me)
+    barrier = pltpu.get_barrier_semaphore()
+    place_here = me % CORES_HERE
+    facing_level = levels - 1 - level
+    for k in range(CORES_HERE):
+        if k:
+            greet(level * CORES_HERE + lax.rem(place_here + k, CORES_HERE))
+        greet(facing_level * CORES_HERE + k)
+    group = 2 * CORES_HERE
+    others = [(1 - near) * (1 + up) + near * (levels - 1) * up for up in range(2)]
+
+    @pl.when(near == 1)
+    def _():
+        pl.semaphore_wait(barrier, group - 1)
+
+    @pl.when(near == 0)
+    def _():
+        pl.semaphore_wait(barrier, devices - 1)
+
+    for up in range(2):
+        for k in range(CORES_HERE):
+            greet(others[up] * CORES_HERE + k)
 
     my_rows = block(me, TILE)
 
-    def send_pair(index):
+    def send_pair(index, start, end):
         def step(i, carry):
             goal = level_at(i // per_level)
             j = lax.rem(i + me, per_level)
@@ -267,12 +284,19 @@
 
             return carry
 
-        lax.fori_loop(0, HEADS, step, 0)
+        lax.fori_loop(start, end, step, 0)
 
     chosen = pltpu.make_async_copy(chosen_ref, place_ref, chosen_sem)
     chosen.start()
-    send_pair(0)
-    send_pair(1)
+    early = near * 2 * per_level
+    send_pair(0, 0, early)
+
+    @pl.when(near == 1)
+    def _():
+        pl.semaphore_wait(barrier, group)
+
+    send_pair(0, early, HEADS)
+    send_pair(1, 0, HEADS)
     chosen.wait()
 
     def find(t, carry):
@@ -419,7 +443,7 @@
                 ]
 
         def send_sums(n, carry):
-            tile = level_at(n // CORES_HERE) * CORES_HERE + lax.rem(n, CORES_HERE)
+            tile = level_at(levels - 1 - n // CORES_HERE) * CORES_HERE + lax.rem(n, CORES_HERE)
             rows = block(tile, TILE)
             send_back(
                 slot,

time: 126 us -> 123 us (0.976)
  the two profiles are of different devices: /device:TPU:3 before, /device:TPU:19 now
where the time goes in v4:
time: 123 us
  Pallas kernels  122 us (99%)
    pallas_call x1, Pallas kernels, fused(): pl.pallas_call(functools.partial(fused_kernel, devices), out_shape=[flat]...  120 us

profile of v4, /device:TPU:19, one launch (start us, length us, event | category | flops | bytes accessed | tf_op | source)
XLA Modules:
  0.0 122.7 jit_solution(6134063187470484875)
XLA Ops:
  0.6 119.9 %exchange_heads.1 = (bf16[128,2560]{1,0:T(8,128)(2,1)S(1)}, bf16[128,2560]{1,0:T(8,128)(2,1)S(1)}, bf16[128,2560]{1,0:T(8,128)(2,1)S(1)}, bf16[128,2560]{1,0:T(8,128)(2,1)S(1)}, f32[20,4,128]{2,1,0:T(4,128)S(1)}) custom-call(s32[8,16]{1,0:T(8,128)} %bitcast.1, bf16[128,2560]{1,0:T(8,128)(2,1)} %k_ref.1, bf16[128,2560]{1,0:T(8,128)(2,1)} %v_ref.1, ...), custom_call_target="tpu_custom_call" | custom-call | tf_op jit(solution)/shard_map/exchange_heads/pallas_call | solution.py:504
  120.6 2.1 %place.1 = (bf16[128,2560]{1,0:T(8,128)(2,1)}, bf16[128,2560]{1,0:T(8,128)(2,1)}, bf16[128,2560]{1,0:T(8,128)(2,1)}, bf16[128,2560]{1,0:T(8,128)(2,1)}, f32[2,2560]{1,0:T(2,128)}, /*index=5*/f32[2,2560]{1,0:T(2,128)}) custom-call(bf16[128,2560]{1,0:T(8,128)(2,1)S(1)} %get-tuple-element.11.a_ref, bf16[128,2560]{1,0:T(8,128)(2,1)S(1)} %get-tuple-element.12.b_ref, ...), custom_call_target="tpu_custom_call" | custom-call | tf_op jit(solution)/shard_map/place/pallas_call | solution.py:573

commit v5 on v4

--- a/solution.py
+++ b/solution.py
@@ -390,10 +390,10 @@
             summit = jnp.max(scores, axis=0, keepdims=True)
             raised = jnp.exp2((scores - summit) * rate)
             scale = 1.0 / jnp.sum(raised, axis=0, keepdims=True)
-            dots = jnp.sum(raised * prob_grad, axis=0, keepdims=True) * scale
             weights = raised * scale
+            rounded = weights.astype(jnp.bfloat16)
+            dots = jnp.sum(rounded.astype(jnp.float32) * prob_grad, axis=0, keepdims=True)
             score_grad = (weights * (prob_grad - dots)).astype(jnp.bfloat16)
-            rounded = weights.astype(jnp.bfloat16)
             for part, values in ((0, score_grad), (HEAD_DIM, rounded)):
                 for j in range(SEL):
                     kept[i, j, :, part : part + HEAD_DIM] = values[j * TILE : (j + 1) * TILE]
@@ -443,7 +443,8 @@
                 ]
 
         def send_sums(n, carry):
-            tile = level_at(levels - 1 - n // CORES_HERE) * CORES_HERE + lax.rem(n, CORES_HERE)
+            goal = level_at(levels - 1 - n // CORES_HERE)
+            tile = goal * CORES_HERE + lax.rem(n + me, CORES_HERE)
             rows = block(tile, TILE)
             send_back(
                 slot,

time: 123 us -> 123 us (level)
  the two profiles are of different devices: /device:TPU:19 before, /device:TPU:17 now
where the time goes in v5:
time: 123 us
  Pallas kernels  122 us (99%)
    pallas_call x1, Pallas kernels, fused(): pl.pallas_call(functools.partial(fused_kernel, devices), out_shape=[flat]...  120 us

profile of v5, /device:TPU:17, one launch (start us, length us, event | category | flops | bytes accessed | tf_op | source)
XLA Modules:
  0.0 122.9 jit_solution(820930943082792058)
XLA Ops:
  0.6 120.1 %exchange_heads.1 = (bf16[128,2560]{1,0:T(8,128)(2,1)S(1)}, bf16[128,2560]{1,0:T(8,128)(2,1)S(1)}, bf16[128,2560]{1,0:T(8,128)(2,1)S(1)}, bf16[128,2560]{1,0:T(8,128)(2,1)S(1)}, f32[20,4,128]{2,1,0:T(4,128)S(1)}) custom-call(s32[8,16]{1,0:T(8,128)} %bitcast.1, bf16[128,2560]{1,0:T(8,128)(2,1)} %k_ref.1, bf16[128,2560]{1,0:T(8,128)(2,1)} %v_ref.1, ...), custom_call_target="tpu_custom_call" | custom-call | tf_op jit(solution)/shard_map/exchange_heads/pallas_call | solution.py:505
  120.8 2.1 %place.1 = (bf16[128,2560]{1,0:T(8,128)(2,1)}, bf16[128,2560]{1,0:T(8,128)(2,1)}, bf16[128,2560]{1,0:T(8,128)(2,1)}, bf16[128,2560]{1,0:T(8,128)(2,1)}, f32[2,2560]{1,0:T(2,128)}, /*index=5*/f32[2,2560]{1,0:T(2,128)}) custom-call(bf16[128,2560]{1,0:T(8,128)(2,1)S(1)} %get-tuple-element.11.a_ref, bf16[128,2560]{1,0:T(8,128)(2,1)S(1)} %get-tuple-element.12.b_ref, ...), custom_call_target="tpu_custom_call" | custom-call | tf_op jit(solution)/shard_map/place/pallas_call | solution.py:574
